TPU v7x, 32 devices: a whole 2x2x4 slice. The times are simulated.
32 devices in a mesh: dp: 4 (over y, x), tensor: 8 (over z, core).
Axes of the slice: x: 2, y: 2, z: 4, core: 2. Of those that a mesh axis runs over, the one named last changes fastest.
Arguments:
- queries: bfloat16 [1536, 8192], P('dp', 'tensor'), may hold values from -180 to 180
- keys: bfloat16 [1536, 1024], P('dp'), may hold values from -4.5 to 4.5
- values: bfloat16 [1536, 1024], P('dp'), may hold values from -6 to 6
- grad_out: bfloat16 [1536, 8192], P('dp', 'tensor'), may hold values from -3 to 3
- weight: float32 [8192, 8192], P('dp', 'tensor'), as said below
- first_code: bfloat16 [8192, 8192], P('dp', 'tensor'), may hold values from -1 to 1, as said below
- first_rows: float32 [8192], P('dp'), may hold values from 0.2 to 5
- first_cols: float32 [8192], P('tensor'), may hold values from 0.2 to 5
- second_code: bfloat16 [8192, 8192], P('dp', 'tensor'), may hold values from 0 to 1, as said below
- second_rows: float32 [8192], P('dp'), may hold values from 0.5 to 20
- second_cols: float32 [8192], P('tensor'), may hold values from 0.5 to 20
Outputs:
- grad_queries: bfloat16 [1536, 8192], P('dp', 'tensor')
- new_weight: float32 [8192, 8192], P('dp', 'tensor')
- next_first_code: bfloat16 [8192, 8192], P('dp', 'tensor')
- next_first_rows: float32 [8192], P('dp')
- next_first_cols: float32 [8192], P('tensor')
- next_second_code: bfloat16 [8192, 8192], P('dp', 'tensor')
- next_second_rows: float32 [8192], P('dp')
- next_second_cols: float32 [8192], P('tensor')
Inputs may be any that keep to these rules, and one draw needn't show every extreme that they name: `weight`: rows 8192 onward are zero. `first_code`: rows 8192 onward are zero. `second_code`: rows 8192 onward are zero; all other entries are 0.05 or more.
All inputs are finite; a program needn't handle non-finite values.
Results may differ from a plain program's by a relative error of at most 0.023.
Values may be sent and summed in bfloat16 or wider, within the bound.
A program may use at most 128 MiB of HBM per device.

v0:
```python
import jax
import jax.numpy as jnp
from jax import lax
from jax.sharding import PartitionSpec as P

H = 64
KVH = 8
HD = 128


beta_first = 0.9
beta_second = 0.95
learning = 0.01
decay_rate = 0.1
adam_eps = 1e-08
code_eps = 1e-06
correct_first = 1.0 - 0.9**10
correct_second = 1.0 - 0.95**10


def attend(queries, key_sel, value_sel, heads_dev):
    length = queries.shape[0]
    query_heads = queries.reshape(length, heads_dev, HD)
    scores = jnp.einsum(
        "qhd,kd->hqk", query_heads, key_sel, preferred_element_type=jnp.float32
    ) * HD ** (-0.5)
    future = lax.broadcasted_iota(jnp.int32, (length, length), 1) > lax.broadcasted_iota(
        jnp.int32, (length, length), 0
    )
    scores = jnp.where(future[None], -1e30, scores)
    highest = jnp.max(scores, axis=-1, keepdims=True)
    exponent = jnp.exp(scores - highest)
    probabilities = exponent / jnp.sum(exponent, axis=-1, keepdims=True)
    weights_half = probabilities.astype(jnp.bfloat16)
    attended = jnp.einsum(
        "hqk,kd->qhd", weights_half, value_sel, preferred_element_type=jnp.float32
    )
    return (probabilities, attended.astype(jnp.bfloat16).reshape(length, heads_dev * HD))


def attend_back(probabilities, attended, grad_half, key_sel, value_sel, heads_dev):
    length = grad_half.shape[0]
    grad_heads = grad_half.reshape(length, heads_dev, HD)
    grad_probs = jnp.einsum(
        "qhd,kd->hqk", grad_heads, value_sel, preferred_element_type=jnp.float32
    )
    row_dot = jnp.sum(
        grad_heads.astype(jnp.float32)
        * attended.reshape(length, heads_dev, HD).astype(jnp.float32),
        axis=-1,
    )
    grad_scores = (probabilities * (grad_probs - row_dot.T[:, :, None])).astype(jnp.bfloat16)
    grad_query = jnp.einsum(
        "hqk,kd->qhd", grad_scores, key_sel, preferred_element_type=jnp.float32
    ) * HD ** (-0.5)
    return grad_query.astype(jnp.bfloat16).reshape(length, heads_dev * HD)


def per_device(
    queries,
    keys,
    values,
    grad_out,
    weight,
    first_code,
    first_rows,
    first_cols,
    second_code,
    second_rows,
    second_cols,
):
    dp_count = lax.axis_size("dp")
    cols_dev = queries.shape[1]
    heads_dev = cols_dev // HD
    rows_dev = weight.shape[0]
    width_pad = dp_count * rows_dev
    tensor_index = lax.axis_index("tensor")
    kv_start = tensor_index * heads_dev // (H // KVH) * HD
    weight_half = weight.astype(jnp.bfloat16)
    full_grad = lax.all_gather(grad_out, "tensor", axis=1, tiled=True)
    padded = jnp.pad(full_grad, ((0, 0), (0, width_pad - full_grad.shape[1])))
    key_sel = lax.dynamic_slice_in_dim(keys, kv_start, HD, 1)
    value_sel = lax.dynamic_slice_in_dim(values, kv_start, HD, 1)
    probabilities, attended = attend(queries, key_sel, value_sel, heads_dev)
    block = padded
    grad_att = jnp.dot(
        block,
        lax.all_gather(weight_half, "dp", axis=0, tiled=True),
        preferred_element_type=jnp.float32,
    )
    block = padded
    weight_grad = lax.psum_scatter(
        jnp.einsum("sc,sh->ch", block, attended, preferred_element_type=jnp.float32).astype(
            jnp.bfloat16
        ),
        "dp",
        scatter_dimension=0,
        tiled=True,
    ).astype(jnp.float32)
    grad_half = grad_att.astype(jnp.bfloat16)
    grad_queries = attend_back(probabilities, attended, grad_half, key_sel, value_sel, heads_dev)
    first = first_code.astype(jnp.float32) * jnp.minimum(first_rows[:, None], first_cols[None, :])
    second = second_code.astype(jnp.float32) * jnp.minimum(
        second_rows[:, None], second_cols[None, :]
    )
    first_new = beta_first * first + (1.0 - beta_first) * weight_grad
    second_new = beta_second * second + (1.0 - beta_second) * weight_grad * weight_grad
    step_size = first_new / correct_first / (jnp.sqrt(second_new / correct_second) + adam_eps)
    new_weight = weight - learning * (step_size + decay_rate * weight)
    first_abs = jnp.abs(first_new)
    second_abs = jnp.abs(second_new)
    local_rows_max = jnp.stack([jnp.max(first_abs, axis=1), jnp.max(second_abs, axis=1)])
    local_cols_max = jnp.stack([jnp.max(first_abs, axis=0), jnp.max(second_abs, axis=0)])
    rows_mine = lax.pmax(local_rows_max, "tensor")
    cols_mine = lax.pmax(local_cols_max, "dp")
    next_first_code = (
        first_new / (jnp.minimum(rows_mine[0][:, None], cols_mine[0][None, :]) + code_eps)
    ).astype(jnp.bfloat16)
    next_second_code = (
        second_new / (jnp.minimum(rows_mine[1][:, None], cols_mine[1][None, :]) + code_eps)
    ).astype(jnp.bfloat16)
    return (
        grad_queries,
        new_weight,
        next_first_code,
        rows_mine[0],
        cols_mine[0],
        next_second_code,
        rows_mine[1],
        cols_mine[1],
    )


def solution(mesh):
    return jax.shard_map(
        per_device,
        mesh=mesh,
        in_specs=(
            P("dp", "tensor"),
            P("dp", None),
            P("dp", None),
            P("dp", "tensor"),
            P("dp", "tensor"),
            P("dp", "tensor"),
            P("dp"),
            P("tensor"),
            P("dp", "tensor"),
            P("dp"),
            P("tensor"),
        ),
        out_specs=(
            P("dp", "tensor"),
            P("dp", "tensor"),
            P("dp", "tensor"),
            P("dp"),
            P("tensor"),
            P("dp", "tensor"),
            P("dp"),
            P("tensor"),
        ),
        check_vma=False,
    )
```

profile of v0, /device:TPU:0, one launch (start us, length us, event | category | flops | bytes accessed | tf_op | source)
XLA Modules:
  0.0 510.6 jit_solution(8589471572485193456)
XLA Ops:
  7.2 0.7 all-gather.3.cloned.1.call-update
  8.0 6.1 %convert_element_type.51 = bf16[2048,1024]{1,0:T(8,128)(2,1)} convert(f32[2048,1024]{1,0:T(8,128)} %param.15) | non-fusion elementwise | flops 2097152 | bytes 12582912 | tf_op jit(solution)/shard_map/convert_element_type | solution.py:79
  14.1 0.0 reduce-scatter.2.cloned.1.call-start
  14.3 0.8 fusion.21
  15.1 3.7 fusion.42
  18.7 58.3 %all-gather.3.cloned.1.call-done = bf16[384,8192]{1,0:T(8,128)(2,1)} async-done(((bf16[384,1024]{1,0:T(8,128)(2,1)}), bf16[384,8192]{1,0:T(8,128)(2,1)}) %all-gather.3.cloned.1.call-update) | async-done | bytes 6291472 | tf_op jit(solution)/shard_map/all_gather | solution.py:80
  77.0 158.4 %all-gather.5.cloned.1.call-done = bf16[8192,1024]{1,0:T(8,128)(2,1)} async-done(((bf16[2048,1024]{1,0:T(8,128)(2,1)}), bf16[8192,1024]{1,0:T(8,128)(2,1)}) %all-gather.5.cloned.1.call-update) | async-done | bytes 16777232 | tf_op jit(solution)/shard_map/all_gather | solution.py:88
  235.4 12.1 %convolution_convert_fusion = bf16[384,1024]{1,0:T(8,128)(2,1)S(1)} fusion(bf16[384,8192]{1,0:T(8,128)(2,1)} %all-gather.3.cloned.1.call-done, bf16[8192,1024]{1,0:T(8,128)(2,1)} %all-gather.5.cloned.1.call-done), kind=kOutput, calls=%fused_computation.30 | convolution fusion | flops 6442844160 | bytes 23855104 | tf_op jit(solution)/shard_map/dot_general | solution.py:86
  247.5 0.4 copy.37
  247.9 3.0 multiply_reduce_fusion
  250.9 14.5 %convert_bitcast_fusion = bf16[8192,1024]{0,1:T(8,128)(2,1)} fusion(bf16[384,1024]{0,1:T(8,128)(2,1)S(1)} %bitcast.82, bf16[384,8192]{1,0:T(8,128)(2,1)} %all-gather.3.cloned.1.call-done), kind=kOutput, calls=%fused_computation.1 | convolution fusion | flops 6450839552 | bytes 23855104 | tf_op jit(solution)/shard_map/sc,sh->ch/dot_general | solution.py:93
  265.4 9.4 %copy.28 = f32[2048,1024]{0,1:T(8,128)} copy(f32[2048,1024]{1,0:T(8,128)} %param.15) | data formatting | bytes 16777216 | tf_op args[4]
  274.8 6.4 %copy.25 = bf16[2048,1024]{0,1:T(8,128)(2,1)} copy(bf16[2048,1024]{1,0:T(8,128)(2,1)} %param.16) | data formatting | bytes 8388608 | tf_op args[5]
  281.2 6.5 %copy.26 = bf16[2048,1024]{0,1:T(8,128)(2,1)} copy(bf16[2048,1024]{1,0:T(8,128)(2,1)} %param.19) | data formatting | bytes 8388608 | tf_op args[8]
  287.7 3.7 multiply_convert_fusion
  291.5 1.2 copy.29
  292.6 126.6 %reduce-scatter.2.cloned.1.call-done = bf16[2048,1024]{0,1:T(8,128)(2,1)} async-done(((bf16[8192,1024]{0,1:T(8,128)(2,1)}), bf16[2048,1024]{0,1:T(8,128)(2,1)}) %reduce-scatter.2.cloned.1.call-update) | async-done | bytes 4194320 | tf_op jit(solution)/shard_map/reduce_scatter | solution.py:92
  419.3 15.6 %abs_reduce_fusion.3 = (f32[2048]{0:T(1024)S(1)}, f32[1024]{0:T(1024)S(1)}, f32[1024]{0:T(1024)S(1)}, f32[2048]{0:T(1024)S(1)}, f32[2048,1024]{0,1:T(8,128)}) fusion(bf16[2048,1024]{0,1:T(8,128)(2,1)} %reduce-scatter.2.cloned.1.call-done, f32[1024]{0:T(1024)S(1)} %copy-done.8, f32[2048]{0:T(1024)S(1)} %copy-done.4, bf16[2048,1024]{0,1:T(8,128)(2,1)} %copy.25, ...), kind=kLoop, calls=%fused_computation.12 | loop fusion | flops 58714112 | bytes 29409280 | tf_op jit(solution)/shard_map/reduce_max | solution.py:112
  434.9 9.2 %copy.30 = f32[2048,1024]{1,0:T(8,128)} copy(f32[2048,1024]{0,1:T(8,128)} %get-tuple-element.22) | data formatting | bytes 16777216
  444.2 9.1 %pmax.15 = f32[2,1024]{1,0:T(2,128)S(1)} all-reduce(f32[2,1024]{1,0:T(2,128)S(1)} %pad_maximum_fusion.1), channel_id=1, replica_groups=mesh['dp'=4,'tensor'=8] {'dp'}, use_global_device_ids=true, to_apply=%region_9.10 | all-reduce | flops 2048 | bytes 16384 | tf_op jit(solution)/shard_map/pmax | solution.py:115
  453.4 26.4 %pmax.14 = f32[2,2048]{1,0:T(2,128)S(1)} all-reduce(f32[2,2048]{1,0:T(2,128)S(1)} %pad_maximum_fusion), channel_id=1, replica_groups=mesh['dp'=4,'tensor'=8] {'tensor'}, use_global_device_ids=true, to_apply=%region_6.7 | all-reduce | flops 4096 | bytes 32768 | tf_op jit(solution)/shard_map/pmax | solution.py:114
  479.7 11.5 %divide_convert_fusion = (bf16[2048,1024]{0,1:T(8,128)(2,1)}, bf16[2048,1024]{0,1:T(8,128)(2,1)}) fusion(f32[1024]{0:T(1024)S(1)} %bitcast.76, f32[2048]{0:T(1024)S(1)} %bitcast.70, bf16[2048,1024]{0,1:T(8,128)(2,1)} %reduce-scatter.2.cloned.1.call-done, f32[1024]{0:T(1024)S(1)} %copy-done.9, f32[2048]{0:T(1024)S(1)} %copy-done.5, ...), kind=kLoop, calls=%fused_computation.6 | loop fusion | flops 46137344 | bytes 21020672 | tf_op jit(solution)/shard_map/convert_element_type | solution.py:121
  491.3 6.4 %copy.31 = bf16[2048,1024]{1,0:T(8,128)(2,1)} copy(bf16[2048,1024]{0,1:T(8,128)(2,1)} %get-tuple-element.24) | data formatting | bytes 8388608
  497.7 6.4 %copy.32 = bf16[2048,1024]{1,0:T(8,128)(2,1)} copy(bf16[2048,1024]{0,1:T(8,128)(2,1)} %get-tuple-element.23) | data formatting | bytes 8388608
  (29 shorter events, 0.3 us)
Async XLA Ops:
  7.2 7.1 %copy-start = (bf16[384,1024]{1,0:T(8,128)(2,1)S(1)}, bf16[384,1024]{1,0:T(8,128)(2,1)}, u32[]{:S(2)}) copy-start(bf16[384,1024]{1,0:T(8,128)(2,1)} %param.12) | copy-start | bytes 2359300
  7.2 69.9 %all-gather.3.cloned.1.call-start = ((), (), s32[]{:S(2)}) async-start(), calls=%async_computation.1 | async-start | bytes 7077888 | tf_op jit(solution)/shard_map/all_gather | solution.py:80
  7.9 6.3 %copy-start.1 = (bf16[384,1024]{1,0:T(8,128)(2,1)S(1)}, bf16[384,1024]{1,0:T(8,128)(2,1)}, u32[]{:S(2)}) copy-start(bf16[384,1024]{1,0:T(8,128)(2,1)} %param.11) | copy-start | bytes 2359300
  7.9 227.5 %all-gather.5.cloned.1.call-start = ((), (), s32[]{:S(2)}) async-start(), calls=%async_computation.2 | async-start | bytes 20971520 | tf_op jit(solution)/shard_map/all_gather | solution.py:88
  14.1 405.2 %reduce-scatter.2.cloned.1.call-start = ((), (), s32[]{:S(2)}) async-start(), calls=%async_computation.3 | async-start | bytes 20971520 | tf_op jit(solution)/shard_map/reduce_scatter | solution.py:92
  287.7 131.6 %copy-start.4 = (f32[2048]{0:T(1024)S(1)}, f32[2048]{0:T(1024)}, u32[]{:S(2)}) copy-start(f32[2048]{0:T(1024)} %param.17) | copy-start | bytes 24580
  287.7 131.6 %copy-start.5 = (f32[2048]{0:T(1024)S(1)}, f32[2048]{0:T(1024)}, u32[]{:S(2)}) copy-start(f32[2048]{0:T(1024)} %param.20) | copy-start | bytes 24580
  287.7 131.6 %copy-start.8 = (f32[1024]{0:T(1024)S(1)}, f32[1024]{0:T(1024)}, u32[]{:S(2)}) copy-start(f32[1024]{0:T(1024)} %param.18) | copy-start | bytes 12292
  287.7 131.6 %copy-start.9 = (f32[1024]{0:T(1024)S(1)}, f32[1024]{0:T(1024)}, u32[]{:S(2)}) copy-start(f32[1024]{0:T(1024)} %param.21) | copy-start | bytes 12292
  453.3 38.0 %copy-start.6 = (f32[1,1024]{1,0:T(1,128)}, f32[1,1024]{1,0:T(1,128)S(1)}, u32[]{:S(2)}) copy-start(f32[1,1024]{1,0:T(1,128)S(1)} %get-tuple-element.27) | copy-start | bytes 12292
  453.3 37.9 %copy-start.7 = (f32[1,1024]{1,0:T(1,128)}, f32[1,1024]{1,0:T(1,128)S(1)}, u32[]{:S(2)}) copy-start(f32[1,1024]{1,0:T(1,128)S(1)} %get-tuple-element.28) | copy-start | bytes 12292
  479.7 11.5 %copy-start.2 = (f32[1,2048]{1,0:T(1,128)}, f32[1,2048]{1,0:T(1,128)S(1)}, u32[]{:S(2)}) copy-start(f32[1,2048]{1,0:T(1,128)S(1)} %get-tuple-element.25) | copy-start | bytes 24580
  479.7 11.5 %copy-start.3 = (f32[1,2048]{1,0:T(1,128)}, f32[1,2048]{1,0:T(1,128)S(1)}, u32[]{:S(2)}) copy-start(f32[1,2048]{1,0:T(1,128)S(1)} %get-tuple-element.26) | copy-start | bytes 24580
Sparse Core Ops, SparseCore 0:
  9.6 67.4 all-gather.2
  79.5 155.9 all-gather.4
  265.5 153.7 reduce-scatter.1
where the time goes:
time: 512 us; the launch traced here: 511 us
  waiting for transfers between devices  344 us (67%)
  local copies, waits for them, and re-layouts  46 us (9%)
  other arithmetic  37 us (7%)
  blocking collectives  35.4 us (7%)
  matrix products  34.1 us (7%)
  between operations  13.9 us (3%)
    all_gather x1, waiting for transfers between devices, per_device(): lax.all_gather(weight_half, 'dp', axis=0, tiled=True)  158 us
    reduce_scatter x1, waiting for transfers between devices, per_device(): lax.psum_scatter(jnp.einsum('sc,sh->ch', block, attended, preferred_eleme...  127 us
    all_gather x1, waiting for transfers between devices, per_device(): full_grad = lax.all_gather(grad_out, 'tensor', axis=1, tiled=True)  58.3 us
    unnamed x27, local copies, waits for them, and re-layouts  45.6 us
    pmax x1, blocking collectives, per_device(): rows_mine = lax.pmax(local_rows_max, 'tensor')  26.4 us
    reduce_max x1, other arithmetic, per_device(): jnp.max(first_abs, axis=1)  15.6 us
    dot_general x1, matrix products, per_device(): jnp.einsum('sc,sh->ch', block, attended, preferred_element_type=jnp.float32)  14.5 us
    dot_general x1, matrix products, per_device(): jnp.dot(block, lax.all_gather(weight_half, 'dp', axis=0, tiled=True), pre...  12.1 us
  transfers between devices with their start and end apart: 3, of which 3 were waited for; matrix products, arithmetic and copies ran while one was open for 7% of the time, Pallas kernels for 0%

commit v1 on v0

--- a/solution.py
+++ b/solution.py
@@ -77,27 +77,40 @@
     tensor_index = lax.axis_index("tensor")
     kv_start = tensor_index * heads_dev // (H // KVH) * HD
     weight_half = weight.astype(jnp.bfloat16)
-    full_grad = lax.all_gather(grad_out, "tensor", axis=1, tiled=True)
-    padded = jnp.pad(full_grad, ((0, 0), (0, width_pad - full_grad.shape[1])))
+    length = queries.shape[0]
+    gathered = lax.all_gather(grad_out, "tensor", axis=0)
+    tensor_count, unused, feats = gathered.shape
+    if rows_dev % feats == 0 and width_pad == tensor_count * feats:
+        pieces = rows_dev // feats
+        blocks = gathered.reshape(dp_count, pieces, length, feats)
+    else:
+        pieces = 1
+        flat = jnp.moveaxis(gathered, 0, 1).reshape(length, tensor_count * feats)
+        flat = jnp.pad(flat, ((0, 0), (0, width_pad - flat.shape[1])))
+        blocks = jnp.moveaxis(flat.reshape(length, dp_count, 1, rows_dev), 0, 2)
     key_sel = lax.dynamic_slice_in_dim(keys, kv_start, HD, 1)
     value_sel = lax.dynamic_slice_in_dim(values, kv_start, HD, 1)
     probabilities, attended = attend(queries, key_sel, value_sel, heads_dev)
-    block = padded
-    grad_att = jnp.dot(
-        block,
-        lax.all_gather(weight_half, "dp", axis=0, tiled=True),
-        preferred_element_type=jnp.float32,
+    all_attended = lax.all_gather(attended, "dp", axis=0, tiled=True)
+    mine = lax.all_to_all(blocks, "dp", 0, 0, tiled=True)
+    span = rows_dev // pieces
+    parts = [mine[:, k].reshape(dp_count * length, span) for k in range(pieces)]
+    partial = sum(
+        jnp.dot(
+            parts[k], weight_half[k * span : (k + 1) * span], preferred_element_type=jnp.float32
+        )
+        for k in range(pieces)
     )
-    block = padded
-    weight_grad = lax.psum_scatter(
-        jnp.einsum("sc,sh->ch", block, attended, preferred_element_type=jnp.float32).astype(
-            jnp.bfloat16
-        ),
-        "dp",
-        scatter_dimension=0,
-        tiled=True,
-    ).astype(jnp.float32)
-    grad_half = grad_att.astype(jnp.bfloat16)
+    grad_half = lax.psum_scatter(
+        partial.astype(jnp.bfloat16), "dp", scatter_dimension=0, tiled=True
+    )
+    weight_grad = jnp.concatenate(
+        [
+            jnp.einsum("sc,sh->ch", parts[k], all_attended, preferred_element_type=jnp.float32)
+            for k in range(pieces)
+        ],
+        axis=0,
+    )
     grad_queries = attend_back(probabilities, attended, grad_half, key_sel, value_sel, heads_dev)
     first = first_code.astype(jnp.float32) * jnp.minimum(first_rows[:, None], first_cols[None, :])
     second = second_code.astype(jnp.float32) * jnp.minimum(

time: 512 us -> 330 us (0.64)
  waiting for transfers between devices: 344 us -> 197 us
  local copies, waits for them, and re-layouts: 46 us -> 9.33 us
  matrix products: 34.1 us -> 28.3 us
  starting transfers between devices: 0.12 us -> 5.54 us
    all_gather x2, waiting for transfers between devices: 217 us -> 63.3 us  [the longest x1 63.3 us: per_device(): gathered = lax.all_gather(grad_out, 'tensor', axis=0)]
    all_to_all x0 -> x1, waiting for transfers between devices: none -> 91.6 us  [per_device(): mine = lax.all_to_all(blocks, 'dp', 0, 0, tiled=True)]
    reduce_scatter x1, waiting for transfers between devices: 127 us -> 41.1 us  [per_device(): lax.psum_scatter(partial.astype(jnp.bfloat16), 'dp', scatter_dimension=0,...]
    unnamed x27 -> x33, local copies, waits for them, and re-layouts: 45.6 us -> 1.58 us
    convert_element_type x1, other arithmetic: 11.5 us -> 23.6 us  [per_device(): next_second_code = (second_new / (jnp.minimum(rows_mine[1][:, None], cols...]
    dot_general x2 -> x4, matrix products: 26.5 us -> 18.8 us  [the longest x2 10.2 us: per_device(): jnp.einsum('sc,sh->ch', parts[k], all_attended, preferred_element_type=jn...]
    slice x0 -> x1, local copies, waits for them, and re-layouts: none -> 6.24 us  [per_device(): parts = [mine[:, k].reshape(dp_count * length, span) for k in range(pieces)]]
    convert_element_type x1 -> x0, other arithmetic: 6.13 us -> none  [per_device(): weight_half = weight.astype(jnp.bfloat16)]
  transfers between devices with their start and end apart: 3 -> 4, of which waited for: 3 -> 3; matrix products, arithmetic and copies ran while one was open for 7% -> 5% of each run, Pallas kernels for 0% -> 0%
where the time goes in v1:
time: 330 us; the launch traced here: 329 us
  waiting for transfers between devices  197 us (60%)
  other arithmetic  38.4 us (12%)
  blocking collectives  35.2 us (11%)
  matrix products  28.3 us (9%)
  between operations  15.8 us (5%)
  local copies, waits for them, and re-layouts  9.33 us (3%)
  starting transfers between devices  5.54 us (2%)
    all_to_all x1, waiting for transfers between devices, per_device(): mine = lax.all_to_all(blocks, 'dp', 0, 0, tiled=True)  91.6 us
    all_gather x1, waiting for transfers between devices, per_device(): gathered = lax.all_gather(grad_out, 'tensor', axis=0)  63.3 us
    reduce_scatter x1, waiting for transfers between devices, per_device(): lax.psum_scatter(partial.astype(jnp.bfloat16), 'dp', scatter_dimension=0,...  41.1 us
    pmax x1, blocking collectives, per_device(): rows_mine = lax.pmax(local_rows_max, 'tensor')  25.9 us
    convert_element_type x1, other arithmetic, per_device(): next_second_code = (second_new / (jnp.minimum(rows_mine[1][:, None], cols...  23.6 us
    reduce_max x1, other arithmetic, per_device(): jnp.max(first_abs, axis=1)  10.9 us
    dot_general x2, matrix products, per_device(): jnp.einsum('sc,sh->ch', parts[k], all_attended, preferred_element_type=jn...  10.2 us
    pmax x1, blocking collectives, per_device(): cols_mine = lax.pmax(local_cols_max, 'dp')  9.26 us
  transfers between devices with their start and end apart: 4, of which 3 were waited for; matrix products, arithmetic and copies ran while one was open for 5% of the time, Pallas kernels for 0%

profile of v1, /device:TPU:0, one launch (start us, length us, event | category | flops | bytes accessed | tf_op | source)
XLA Modules:
  0.0 329.2 jit_solution(2072484945500145302)
XLA Ops:
  8.1 0.7 all-gather.6.cloned.1.call-update
  8.8 0.3 copy-done
  9.1 1.9 fusion.23
  11.1 3.6 %fusion.46 = (f32[8,384]{1,0:T(8,128)S(1)}, f32[8,384,384]{1,2,0:T(8,128)}) fusion(f32[384,384,8]{1,0,2:T(8,128)S(1)} %fusion.23, pred[384,384]{0,1:T(8,128)(4,1)S(1)} %iota_compare_fusion), kind=kOutput, calls=%fused_computation.58 | output fusion | flops 7078271 | bytes 9596928 | tf_op jit(solution)/shard_map/sub | solution.py:32
  14.6 63.3 %all-gather.6.cloned.1.call-done = bf16[3072,1024]{1,0:T(8,128)(2,1)} async-done(((bf16[384,1024]{1,0:T(8,128)(2,1)}), bf16[3072,1024]{1,0:T(8,128)(2,1)}) %all-gather.6.cloned.1.call-update) | async-done | bytes 6291472 | tf_op jit(solution)/shard_map/all_gather | solution.py:81
  77.9 5.2 %all-to-all-start = ((bf16[4,2,384,1024]{3,2,1,0:T(8,128)(2,1)}), bf16[4,2,384,1024]{3,2,1,0:T(8,128)(2,1)}, u32[]{:S(2)}, u32[]{:S(2)}) async-start(bf16[4,2,384,1024]{3,2,1,0:T(8,128)(2,1)} %bitcast.73), calls=%async_computation | async-start | bytes 12582912 | tf_op jit(solution)/shard_map/all_to_all | solution.py:95
  83.2 0.0 all-gather.4.cloned.1.call-start
  83.2 3.9 %fusion.20 = bf16[128,8,384]{2,0,1:T(8,128)(2,1)} fusion(f32[8,384,384]{1,2,0:T(8,128)} %get-tuple-element.36, f32[8,384]{1,0:T(8,128)S(1)} %get-tuple-element.35, bf16[384,1024]{1,0:T(8,128)(2,1)} %param.13, s32[]{:T(128)S(6)} %select_n.14), kind=kOutput, calls=%fused_computation.35 | convolution fusion | flops 304742400 | bytes 5615620 | tf_op jit(solution)/shard_map/hqk,kd->qhd/dot_general | solution.py:35
  87.1 0.2 reduce-scatter.2.cloned.1.call-start
  87.4 91.6 %all-to-all-done = bf16[4,2,384,1024]{3,2,1,0:T(8,128)(2,1)} async-done(((bf16[4,2,384,1024]{3,2,1,0:T(8,128)(2,1)}), bf16[4,2,384,1024]{3,2,1,0:T(8,128)(2,1)}, u32[]{:S(2)}, u32[]{:S(2)}) %all-to-all-start) | async-done | bytes 6291488 | tf_op jit(solution)/shard_map/all_to_all | solution.py:95
  179.0 6.2 %fusion.43 = (bf16[4,1,384,1024]{3,2,1,0:T(8,128)(2,1)}, bf16[4,1,384,1024]{3,2,1,0:T(8,128)(2,1)}) fusion(bf16[4,2,384,1024]{3,2,1,0:T(8,128)(2,1)} %all-to-all-done), kind=kLoop, calls=%fused_computation.55 | loop fusion | bytes 12582912 | tf_op jit(solution)/shard_map/slice | solution.py:97
  185.2 6.6 %convolution_bitcast_fusion = f32[1024,1024]{1,0:T(8,128)S(1)} fusion(bf16[1536,1024]{0,1:T(8,128)(2,1)} %all-gather.4.cloned.1.call-done, bf16[1536,1024]{1,0:T(8,128)(2,1)} %bitcast.76), kind=kOutput, calls=%fused_computation.28 | convolution fusion | flops 3221225472 | bytes 10485760 | tf_op jit(solution)/shard_map/sc,sh->ch/dot_general | solution.py:109
  191.9 3.6 %convolution_bitcast_fusion.1 = f32[1024,1024]{1,0:T(8,128)S(1)} fusion(bf16[1536,1024]{0,1:T(8,128)(2,1)S(1)} %copy-done.15, bf16[1536,1024]{1,0:T(8,128)(2,1)S(1)} %bitcast.78), kind=kOutput, calls=%fused_computation.29 | convolution fusion | flops 3221225472 | bytes 10485760 | tf_op jit(solution)/shard_map/sc,sh->ch/dot_general | solution.py:109
  195.6 10.9 %abs_reduce_fusion.3 = (f32[2048]{0:T(1024)S(1)}, f32[1024]{0:T(1024)S(1)}, f32[2048,1024]{1,0:T(8,128)}, f32[1024]{0:T(1024)S(1)}, f32[2048]{0:T(1024)S(1)}, /*index=5*/f32[2048,1024]{1,0:T(8,128)}) fusion(f32[1024,1024]{1,0:T(8,128)S(1)} %convolution_bitcast_fusion, f32[1024,1024]{1,0:T(8,128)S(1)} %convolution_bitcast_fusion.1, f32[1024]{0:T(1024)S(1)} %copy-done.13, ...), kind=kLoop, calls=%fused_computation.11 | loop fusion | flops 41936896 | bytes 33603584 | tf_op jit(solution)/shard_map/reduce_max | solution.py:125
  206.4 25.9 %pmax.14 = f32[2,2048]{1,0:T(2,128)S(1)} all-reduce(f32[2,2048]{1,0:T(2,128)S(1)} %pad_maximum_fusion.1), channel_id=1, replica_groups=mesh['dp'=4,'tensor'=8] {'tensor'}, use_global_device_ids=true, to_apply=%region_6.7 | all-reduce | flops 4096 | bytes 32768 | tf_op jit(solution)/shard_map/pmax | solution.py:127
  232.4 9.3 %pmax.15 = f32[2,1024]{1,0:T(2,128)S(1)} all-reduce(f32[2,1024]{1,0:T(2,128)S(1)} %pad_maximum_fusion.2), channel_id=1, replica_groups=mesh['dp'=4,'tensor'=8] {'dp'}, use_global_device_ids=true, to_apply=%region_9.10 | all-reduce | flops 2048 | bytes 16384 | tf_op jit(solution)/shard_map/pmax | solution.py:128
  241.7 23.6 %divide_convert_fusion = (bf16[2048,1024]{1,0:T(8,128)(2,1)}, f32[2048,1024]{1,0:T(8,128)}, bf16[2048,1024]{1,0:T(8,128)(2,1)}, bf16[2048,1024]{1,0:T(8,128)(2,1)S(1)}) fusion(f32[2048,1024]{1,0:T(8,128)} %get-tuple-element.28, f32[1024]{0:T(1024)S(1)} %bitcast.87, f32[2048]{0:T(1024)S(1)} %bitcast.81, f32[2048,1024]{1,0:T(8,128)} %param.15, ...), kind=kLoop, calls=%fused_computation.4 | loop fusion | flops 35651584 | bytes 46161920 | tf_op jit(solution)/shard_map/convert_element_type | solution.py:134
  265.4 3.5 %fusion.16 = f32[1536,1024]{1,0:T(8,128)S(1)} fusion(bf16[1536,1024]{1,0:T(8,128)(2,1)S(1)} %bitcast.79, bf16[2048,1024]{1,0:T(8,128)(2,1)S(1)} %get-tuple-element.25), kind=kOutput, calls=%fused_computation.31 | convolution fusion | flops 3221225472 | bytes 11534336 | tf_op jit(solution)/shard_map/dot_general | solution.py:99
  268.9 5.2 %add_convert_fusion = bf16[1536,1024]{1,0:T(8,128)(2,1)} fusion(f32[1536,1024]{1,0:T(8,128)S(1)} %fusion.16, bf16[1536,1024]{1,0:T(8,128)(2,1)S(1)} %bitcast.77, bf16[2048,1024]{1,0:T(8,128)(2,1)S(1)} %get-tuple-element.25), kind=kOutput, calls=%fused_computation.12 | convolution fusion | flops 3224371200 | bytes 14680064 | tf_op jit(solution)/shard_map/dot_general | solution.py:99
  274.1 41.1 %reduce-scatter.2.cloned.1.call-done = bf16[384,1024]{1,0:T(8,128)(2,1)} async-done(((bf16[1536,1024]{1,0:T(8,128)(2,1)}), bf16[384,1024]{1,0:T(8,128)(2,1)}) %reduce-scatter.2.cloned.1.call-update) | async-done | bytes 786448 | tf_op jit(solution)/shard_map/reduce_scatter | solution.py:104
  315.2 1.5 copy.30
  316.7 0.2 multiply_reduce_fusion
  317.0 3.6 %multiply_convert_fusion = bf16[128,8,384]{2,0,1:T(8,128)(2,1)S(1)} fusion(bf16[384,8,128]{0,2,1:T(8,128)(2,1)S(1)} %bitcast.75, f32[8,384]{1,0:T(8,128)S(1)} %bitcast.93, f32[8,384,384]{1,2,0:T(8,128)} %get-tuple-element.36, f32[8,384]{1,0:T(8,128)S(1)} %get-tuple-element.35, bf16[384,1024]{1,0:T(8,128)(2,1)} %param.13, s32[]{:T(128)S(6)} %select_n.14, ...), kind=kOutput, calls=%fused_computation.33 | convolution fusion | flops 609484800 | bytes 6513664 | tf_op jit(solution)/shard_map/hqk,kd->qhd/dot_general | solution.py:53
  320.6 1.2 copy.25
  (40 shorter events, 0.3 us)
Async XLA Ops:
  8.0 1.1 copy-start
  8.0 69.9 %all-gather.6.cloned.1.call-start = ((), (), s32[]{:S(2)}) async-start(), calls=%async_computation.4 | async-start | bytes 7077888 | tf_op jit(solution)/shard_map/all_gather | solution.py:81
  77.9 101.1 %all-to-all-start = ((bf16[4,2,384,1024]{3,2,1,0:T(8,128)(2,1)}), bf16[4,2,384,1024]{3,2,1,0:T(8,128)(2,1)}, u32[]{:S(2)}, u32[]{:S(2)}) async-start(bf16[4,2,384,1024]{3,2,1,0:T(8,128)(2,1)} %bitcast.73), calls=%async_computation | async-start | bytes 12582912 | tf_op jit(solution)/shard_map/all_to_all | solution.py:95
  83.2 102.1 %all-gather.4.cloned.1.call-start = ((), (), s32[]{:S(2)}) async-start(), calls=%async_computation.3 | async-start | bytes 3932160 | tf_op jit(solution)/shard_map/all_gather | solution.py:94
  87.1 228.1 %reduce-scatter.2.cloned.1.call-start = ((), (), s32[]{:S(2)}) async-start(), calls=%async_computation.2 | async-start | bytes 3932160 | tf_op jit(solution)/shard_map/reduce_scatter | solution.py:104
  185.2 6.6 %copy-start.5 = (bf16[4,1,384,1024]{3,2,1,0:T(8,128)(2,1)S(1)}, bf16[4,1,384,1024]{3,2,1,0:T(8,128)(2,1)}, u32[]{:S(2)}) copy-start(bf16[4,1,384,1024]{3,2,1,0:T(8,128)(2,1)} %get-tuple-element.30) | copy-start | bytes 9437188
  185.2 6.6 %copy-start.15 = (bf16[1536,1024]{0,1:T(8,128)(2,1)S(1)}, bf16[1536,1024]{0,1:T(8,128)(2,1)}, u32[]{:S(2)}) copy-start(bf16[1536,1024]{0,1:T(8,128)(2,1)} %all-gather.4.cloned.1.call-done) | copy-start | bytes 9437188
  191.8 3.6 %copy-start.1 = (bf16[2048,1024]{1,0:T(8,128)(2,1)S(1)}, bf16[2048,1024]{1,0:T(8,128)(2,1)}, u32[]{:S(2)}) copy-start(bf16[2048,1024]{1,0:T(8,128)(2,1)} %param.16) | copy-start | bytes 12582916
  191.9 3.6 %copy-start.2 = (bf16[2048,1024]{1,0:T(8,128)(2,1)S(1)}, bf16[2048,1024]{1,0:T(8,128)(2,1)}, u32[]{:S(2)}) copy-start(bf16[2048,1024]{1,0:T(8,128)(2,1)} %param.19) | copy-start | bytes 12582916
  191.9 3.6 %copy-start.11 = (f32[2048]{0:T(1024)S(1)}, f32[2048]{0:T(1024)}, u32[]{:S(2)}) copy-start(f32[2048]{0:T(1024)} %param.17) | copy-start | bytes 24580
  191.9 3.6 %copy-start.12 = (f32[2048]{0:T(1024)S(1)}, f32[2048]{0:T(1024)}, u32[]{:S(2)}) copy-start(f32[2048]{0:T(1024)} %param.20) | copy-start | bytes 24580
  191.9 3.6 %copy-start.13 = (f32[1024]{0:T(1024)S(1)}, f32[1024]{0:T(1024)}, u32[]{:S(2)}) copy-start(f32[1024]{0:T(1024)} %param.18) | copy-start | bytes 12292
  191.9 3.6 %copy-start.14 = (f32[1024]{0:T(1024)S(1)}, f32[1024]{0:T(1024)}, u32[]{:S(2)}) copy-start(f32[1024]{0:T(1024)} %param.21) | copy-start | bytes 12292
  241.6 23.7 %copy-start.9 = (f32[1,1024]{1,0:T(1,128)}, f32[1,1024]{1,0:T(1,128)S(1)}, u32[]{:S(2)}) copy-start(f32[1,1024]{1,0:T(1,128)S(1)} %get-tuple-element.33) | copy-start | bytes 12292
  241.7 23.7 %copy-start.10 = (f32[1,1024]{1,0:T(1,128)}, f32[1,1024]{1,0:T(1,128)S(1)}, u32[]{:S(2)}) copy-start(f32[1,1024]{1,0:T(1,128)S(1)} %get-tuple-element.34) | copy-start | bytes 12292
  241.7 23.7 %copy-start.7 = (f32[1,2048]{1,0:T(1,128)}, f32[1,2048]{1,0:T(1,128)S(1)}, u32[]{:S(2)}) copy-start(f32[1,2048]{1,0:T(1,128)S(1)} %get-tuple-element.31) | copy-start | bytes 24580
  241.7 23.7 %copy-start.8 = (f32[1,2048]{1,0:T(1,128)}, f32[1,2048]{1,0:T(1,128)S(1)}, u32[]{:S(2)}) copy-start(f32[1,2048]{1,0:T(1,128)S(1)} %get-tuple-element.32) | copy-start | bytes 24580
  241.7 23.7 %copy-start.6 = (bf16[4,1,384,1024]{3,2,1,0:T(8,128)(2,1)S(1)}, bf16[4,1,384,1024]{3,2,1,0:T(8,128)(2,1)}, u32[]{:S(2)}) copy-start(bf16[4,1,384,1024]{3,2,1,0:T(8,128)(2,1)} %get-tuple-element.30) | copy-start | bytes 9437188
  265.4 3.5 %copy-start.4 = (bf16[4,1,384,1024]{3,2,1,0:T(8,128)(2,1)S(1)}, bf16[4,1,384,1024]{3,2,1,0:T(8,128)(2,1)}, u32[]{:S(2)}) copy-start(bf16[4,1,384,1024]{3,2,1,0:T(8,128)(2,1)} %get-tuple-element.29) | copy-start | bytes 9437188
  274.1 42.6 %copy-start.3 = (bf16[128,8,384]{2,0,1:T(8,128)(2,1)S(1)}, bf16[128,8,384]{2,0,1:T(8,128)(2,1)}, u32[]{:S(2)}) copy-start(bf16[128,8,384]{2,0,1:T(8,128)(2,1)} %fusion.20) | copy-start | bytes 2359300
Sparse Core Ops, SparseCore 0:
  10.5 67.4 all-gather.5
Sparse Core Ops, SparseCore 1:
  87.2 88.8 all-gather.3
  274.2 41.0 reduce-scatter.1

commit v2 on v1

--- a/solution.py
+++ b/solution.py
@@ -1,6 +1,10 @@
+import functools
+
 import jax
 import jax.numpy as jnp
 from jax import lax
+from jax.experimental import pallas as pl
+from jax.experimental.pallas import tpu as pltpu
 from jax.sharding import PartitionSpec as P
 
 H = 64
@@ -54,6 +58,280 @@
         "hqk,kd->qhd", grad_scores, key_sel, preferred_element_type=jnp.float32
     ) * HD ** (-0.5)
     return grad_query.astype(jnp.bfloat16).reshape(length, heads_dev * HD)
+
+
+CORES = 2
+CHUNKS = 2
+
+
+def exchange_kernel(
+    nd, nz, grad_ref, att_ref, g_ref, a_ref, zbuf,
+    up_send, down_send, z_recv, own_send, d_send, d_recv, p_send, p_recv, a_send, a_recv, local_sem,
+):
+    d = lax.axis_index("dp")
+    t = lax.axis_index("tensor")
+    z = t // CORES
+    c = t % CORES
+    partner = t + 1 - 2 * c
+    rows = grad_ref.shape[0] // CHUNKS
+    has_up = z < nz - 1
+    has_down = z > 0
+    barrier = pltpu.get_barrier_semaphore()
+
+    def greet(**where):
+        pl.semaphore_signal(barrier, inc=1, device_id=where)
+
+    greet(tensor=partner)
+    for o in range(1, nd):
+        greet(dp=(d + o) % nd)
+
+    for o in range(1, nz):
+        greet(tensor=(t + CORES * o) % (CORES * nz))
+    pl.semaphore_wait(barrier, nd + nz - 1)
+
+    def part(ch):
+        return pl.ds(ch * rows, rows)
+
+    def block(zp, ch, own):
+        return grad_ref.at[part(ch)] if own else zbuf.at[zp, part(ch)]
+
+    def up(zp, ch, own):
+        return pltpu.make_async_remote_copy(
+            block(zp, ch, own), zbuf.at[zp, part(ch)], up_send.at[zp, ch], z_recv.at[zp, ch],
+            device_id={"tensor": t + CORES},
+        )
+
+    def down(zp, ch, own):
+        return pltpu.make_async_remote_copy(
+            block(zp, ch, own), zbuf.at[zp, part(ch)], down_send.at[zp, ch], z_recv.at[zp, ch],
+            device_id={"tensor": t - CORES},
+        )
+
+    def to_owner(zp, ch, own):
+        return pltpu.make_async_remote_copy(
+            block(zp, ch, own), g_ref.at[d, c, part(ch)], d_send.at[zp, ch], d_recv.at[d, ch],
+            device_id={"dp": zp},
+        )
+
+    def keep(zp, ch, own):
+        return pltpu.make_async_copy(
+            block(zp, ch, own), g_ref.at[d, c, part(ch)], local_sem.at[ch]
+        )
+
+    def keep_partner(zp, ch, own):
+        return pltpu.make_async_remote_copy(
+            block(zp, ch, own), g_ref.at[d, c, part(ch)], own_send.at[ch], p_recv.at[d, ch],
+            device_id={"tensor": partner},
+        )
+
+    def to_partner(dp, ch):
+        return pltpu.make_async_remote_copy(
+            g_ref.at[dp, c, part(ch)], g_ref.at[dp, c, part(ch)], p_send.at[dp, ch],
+            p_recv.at[dp, ch], device_id={"tensor": partner},
+        )
+
+    def att_copy(o):
+        return pltpu.make_async_remote_copy(
+            att_ref, a_ref.at[d], a_send.at[o], a_recv.at[o], device_id={"dp": (d + o) % nd}
+        )
+
+    def spread(zp, ch, own, act):
+        @pl.when(zp == d)
+        def _():
+            act(keep_partner(zp, ch, own), True)
+            act(keep(zp, ch, own), False)
+
+        @pl.when(zp != d)
+        def _():
+            act(to_owner(zp, ch, own), True)
+
+    def start(copy, remote):
+        copy.start()
+
+    def finish(copy, remote):
+        if remote:
+            copy.wait_send()
+        else:
+            copy.wait()
+
+    for ch in range(CHUNKS):
+
+        @pl.when(has_up)
+        def _():
+            up(z, ch, True).start()
+
+        @pl.when(has_down)
+        def _():
+            down(z, ch, True).start()
+
+        spread(z, ch, True, start)
+    for o in range(1, nd):
+        att_copy(o).start()
+    own_att = pltpu.make_async_copy(att_ref, a_ref.at[d], local_sem.at[CHUNKS])
+    own_att.start()
+
+    for dist in range(1, nz):
+        for ch in range(CHUNKS):
+
+            @pl.when(z - dist >= 0)
+            def _():
+                zp = z - dist
+                down(zp, ch, False).wait_recv()
+
+                @pl.when(has_up)
+                def _():
+                    up(zp, ch, False).start()
+
+                spread(zp, ch, False, start)
+
+            @pl.when(z + dist < nz)
+            def _():
+                zp = z + dist
+                down(zp, ch, False).wait_recv()
+
+                @pl.when(has_down)
+                def _():
+                    down(zp, ch, False).start()
+
+                spread(zp, ch, False, start)
+
+    for ch in range(CHUNKS):
+        for o in range(1, nd):
+            src = (d + o) % nd
+            pltpu.make_async_remote_copy(
+                g_ref.at[src, c, part(ch)], g_ref.at[src, c, part(ch)], p_send.at[src, ch],
+                d_recv.at[src, ch], device_id={"tensor": partner},
+            ).wait_recv()
+            to_partner(src, ch).start()
+
+    own_att.wait()
+    for o in range(1, nd):
+        att_copy(o).wait_send()
+        pltpu.make_async_remote_copy(
+            att_ref, a_ref.at[(d + nd - o) % nd], a_send.at[o], a_recv.at[o],
+            device_id={"dp": (d + o) % nd},
+        ).wait_recv()
+    for ch in range(CHUNKS):
+        for src in range(nd):
+            pltpu.make_async_remote_copy(
+                g_ref.at[src, 1 - c, part(ch)], g_ref.at[src, 1 - c, part(ch)],
+                p_send.at[src, ch], p_recv.at[src, ch], device_id={"tensor": partner},
+            ).wait_recv()
+        for o in range(1, nd):
+            to_partner((d + o) % nd, ch).wait_send()
+
+        @pl.when(has_up)
+        def _():
+            up(z, ch, True).wait_send()
+
+        @pl.when(has_down)
+        def _():
+            down(z, ch, True).wait_send()
+
+        spread(z, ch, True, finish)
+        for dist in range(1, nz):
+
+            @pl.when(z - dist >= 0)
+            def _():
+                @pl.when(has_up)
+                def _():
+                    up(z - dist, ch, False).wait_send()
+
+                spread(z - dist, ch, False, finish)
+
+            @pl.when(z + dist < nz)
+            def _():
+                @pl.when(has_down)
+                def _():
+                    down(z + dist, ch, False).wait_send()
+
+                spread(z + dist, ch, False, finish)
+
+
+def exchange(grad_out, attended, nd, nz):
+    length, feats = grad_out.shape
+    dma = pltpu.SemaphoreType.DMA
+    return pl.pallas_call(
+        functools.partial(exchange_kernel, nd, nz),
+        out_shape=(
+            jax.ShapeDtypeStruct((nd, CORES, length, feats), grad_out.dtype),
+            jax.ShapeDtypeStruct((nd,) + attended.shape, attended.dtype),
+        ),
+        in_specs=[pl.BlockSpec(memory_space=pltpu.VMEM)] * 2,
+        out_specs=(pl.BlockSpec(memory_space=pl.ANY),) * 2,
+        scratch_shapes=[
+            pltpu.VMEM((nz, length, feats), grad_out.dtype),
+            dma((nz, CHUNKS)),
+            dma((nz, CHUNKS)),
+            dma((nz, CHUNKS)),
+            dma((CHUNKS,)),
+            dma((nz, CHUNKS)),
+            dma((nd, CHUNKS)),
+            dma((nd, CHUNKS)),
+            dma((nd, CHUNKS)),
+            dma((nd,)),
+            dma((nd,)),
+            dma((CHUNKS + 1,)),
+        ],
+        compiler_params=pltpu.CompilerParams(collective_id=0, has_side_effects=True),
+    )(grad_out, attended)
+
+
+def maxima_kernel(nd, nt, r_ref, c_ref, ro_ref, co_ref, rbuf, cbuf, rs, rr, cs, cr):
+    d = lax.axis_index("dp")
+    t = lax.axis_index("tensor")
+    barrier = pltpu.get_barrier_semaphore()
+    for o in range(1, nt):
+        pl.semaphore_signal(barrier, inc=1, device_id={"tensor": (t + o) % nt})
+    for o in range(1, nd):
+        pl.semaphore_signal(barrier, inc=1, device_id={"dp": (d + o) % nd})
+    pl.semaphore_wait(barrier, nt + nd - 2)
+    copies = [
+        pltpu.make_async_remote_copy(
+            r_ref, rbuf.at[o], rs.at[o], rr.at[o], device_id={"tensor": (t + o) % nt}
+        )
+        for o in range(1, nt)
+    ] + [
+        pltpu.make_async_remote_copy(
+            c_ref, cbuf.at[o], cs.at[o], cr.at[o], device_id={"dp": (d + o) % nd}
+        )
+        for o in range(1, nd)
+    ]
+    for copy in copies:
+        copy.start()
+    for copy in copies:
+        copy.wait()
+    rows = r_ref[...]
+    for o in range(1, nt):
+        rows = jnp.maximum(rows, rbuf[o])
+    ro_ref[...] = rows
+    cols = c_ref[...]
+    for o in range(1, nd):
+        cols = jnp.maximum(cols, cbuf[o])
+    co_ref[...] = cols
+
+
+def maxima(rows, cols, nd, nt):
+    dma = pltpu.SemaphoreType.DMA
+    vmem = pl.BlockSpec(memory_space=pltpu.VMEM)
+    return pl.pallas_call(
+        functools.partial(maxima_kernel, nd, nt),
+        out_shape=(
+            jax.ShapeDtypeStruct(rows.shape, rows.dtype),
+            jax.ShapeDtypeStruct(cols.shape, cols.dtype),
+        ),
+        in_specs=[vmem] * 2,
+        out_specs=(vmem,) * 2,
+        scratch_shapes=[
+            pltpu.VMEM((nt,) + rows.shape, rows.dtype),
+            pltpu.VMEM((nd,) + cols.shape, cols.dtype),
+            dma((nt,)),
+            dma((nt,)),
+            dma((nd,)),
+            dma((nd,)),
+        ],
+        compiler_params=pltpu.CompilerParams(collective_id=1, has_side_effects=True),
+    )(rows, cols)
 
 
 def per_device(
@@ -78,21 +356,21 @@
     kv_start = tensor_index * heads_dev // (H // KVH) * HD
     weight_half = weight.astype(jnp.bfloat16)
     length = queries.shape[0]
-    gathered = lax.all_gather(grad_out, "tensor", axis=0)
-    tensor_count, unused, feats = gathered.shape
-    if rows_dev % feats == 0 and width_pad == tensor_count * feats:
-        pieces = rows_dev // feats
-        blocks = gathered.reshape(dp_count, pieces, length, feats)
-    else:
-        pieces = 1
-        flat = jnp.moveaxis(gathered, 0, 1).reshape(length, tensor_count * feats)
-        flat = jnp.pad(flat, ((0, 0), (0, width_pad - flat.shape[1])))
-        blocks = jnp.moveaxis(flat.reshape(length, dp_count, 1, rows_dev), 0, 2)
     key_sel = lax.dynamic_slice_in_dim(keys, kv_start, HD, 1)
     value_sel = lax.dynamic_slice_in_dim(values, kv_start, HD, 1)
     probabilities, attended = attend(queries, key_sel, value_sel, heads_dev)
-    all_attended = lax.all_gather(attended, "dp", axis=0, tiled=True)
-    mine = lax.all_to_all(blocks, "dp", 0, 0, tiled=True)
+    tensor_count, feats = lax.axis_size("tensor"), grad_out.shape[1]
+    if rows_dev == CORES * feats and tensor_count == CORES * dp_count and length % 32 == 0:
+        pieces = CORES
+        mine, all_attended = exchange(grad_out, attended, dp_count, tensor_count // CORES)
+        all_attended = all_attended.reshape(dp_count * length, cols_dev)
+    else:
+        pieces = 1
+        flat = lax.all_gather(grad_out, "tensor", axis=1, tiled=True)
+        flat = jnp.pad(flat, ((0, 0), (0, width_pad - flat.shape[1])))
+        blocks = jnp.moveaxis(flat.reshape(length, dp_count, 1, rows_dev), 0, 2)
+        mine = lax.all_to_all(blocks, "dp", 0, 0, tiled=True)
+        all_attended = lax.all_gather(attended, "dp", axis=0, tiled=True)
     span = rows_dev // pieces
     parts = [mine[:, k].reshape(dp_count * length, span) for k in range(pieces)]
     partial = sum(
@@ -101,8 +379,11 @@
         )
         for k in range(pieces)
     )
+    partial, all_attended = lax.optimization_barrier(
+        (partial.astype(jnp.bfloat16), all_attended)
+    )
     grad_half = lax.psum_scatter(
-        partial.astype(jnp.bfloat16), "dp", scatter_dimension=0, tiled=True
+        partial, "dp", scatter_dimension=0, tiled=True
     )
     weight_grad = jnp.concatenate(
         [
@@ -124,8 +405,7 @@
     second_abs = jnp.abs(second_new)
     local_rows_max = jnp.stack([jnp.max(first_abs, axis=1), jnp.max(second_abs, axis=1)])
     local_cols_max = jnp.stack([jnp.max(first_abs, axis=0), jnp.max(second_abs, axis=0)])
-    rows_mine = lax.pmax(local_rows_max, "tensor")
-    cols_mine = lax.pmax(local_cols_max, "dp")
+    rows_mine, cols_mine = maxima(local_rows_max, local_cols_max, dp_count, tensor_count)
     next_first_code = (
         first_new / (jnp.minimum(rows_mine[0][:, None], cols_mine[0][None, :]) + code_eps)
     ).astype(jnp.bfloat16)

time: 330 us -> 185 us (0.56)
  waiting for transfers between devices: 197 us -> 0.04 us
  Pallas kernels: 0 us -> 94.2 us
  blocking collectives: 35.2 us -> 0 us
  starting transfers between devices: 5.54 us -> 0.04 us
  matrix products: 28.3 us -> 24.7 us
    pallas_call x0 -> x2, Pallas kernels: none -> 94.2 us  [the longest x1 76.6 us: exchange(): pl.pallas_call(functools.partial(exchange_kernel, nd, nz), out_shape=(jax...]
    all_to_all x1 -> x0, waiting for transfers between devices: 91.6 us -> none  [per_device(): mine = lax.all_to_all(blocks, 'dp', 0, 0, tiled=True)]
    all_gather x2 -> x0, waiting for transfers between devices: 63.3 us -> none  [the longest x1 63.3 us: per_device(): gathered = lax.all_gather(grad_out, 'tensor', axis=0)]
    reduce_scatter x1, waiting for transfers between devices: 41.1 us -> 0.02 us  [per_device(): grad_half = lax.psum_scatter(partial, 'dp', scatter_dimension=0, tiled=True)]
    pmax x2 -> x0, blocking collectives: 35.2 us -> none  [the longest x1 25.9 us: per_device(): rows_mine = lax.pmax(local_rows_max, 'tensor')]
    convert_element_type x0 -> x1, other arithmetic: none -> 6.16 us  [per_device(): weight_half = weight.astype(jnp.bfloat16)]
    all_to_all x1 -> x0, starting transfers between devices: 5.23 us -> none  [per_device(): mine = lax.all_to_all(blocks, 'dp', 0, 0, tiled=True)]
  transfers between devices with their start and end apart: 4 -> 1, of which waited for: 3 -> 0; matrix products, arithmetic and copies ran while one was open for 5% -> 24% of each run, Pallas kernels for 0% -> 10%
where the time goes in v2:
time: 185 us; the launch traced here: 184 us
  Pallas kernels  94.2 us (51%)
  other arithmetic  40.6 us (22%)
  matrix products  24.7 us (13%)
  between operations  14.4 us (8%)
  local copies, waits for them, and re-layouts  10.2 us (6%)
    pallas_call x1, Pallas kernels, exchange(): pl.pallas_call(functools.partial(exchange_kernel, nd, nz), out_shape=(jax...  76.6 us
    convert_element_type x1, other arithmetic, per_device(): next_second_code = (second_new / (jnp.minimum(rows_mine[1][:, None], cols...  20.5 us
    pallas_call x1, Pallas kernels, maxima(): pl.pallas_call(functools.partial(maxima_kernel, nd, nt), out_shape=(jax.S...  17.5 us
    reduce_max x1, other arithmetic, per_device(): jnp.max(first_abs, axis=0)  10.8 us
    dot_general x2, matrix products, per_device(): jnp.einsum('sc,sh->ch', parts[k], all_attended, preferred_element_type=jn...  10.1 us
    dot_general x2, matrix products, per_device(): jnp.dot(parts[k], weight_half[k * span:(k + 1) * span], preferred_element...  8.57 us
    convert_element_type x1, other arithmetic, per_device(): weight_half = weight.astype(jnp.bfloat16)  6.16 us
    slice x1, local copies, waits for them, and re-layouts, per_device(): parts = [mine[:, k].reshape(dp_count * length, span) for k in range(pieces)]  4.21 us
  transfers between devices with their start and end apart: 1, of which 0 were waited for; matrix products, arithmetic and copies ran while one was open for 24% of the time, Pallas kernels for 10%

profile of v2, /device:TPU:0, one launch (start us, length us, event | category | flops | bytes accessed | tf_op | source)
XLA Modules:
  0.0 184.2 jit_solution(16987529732845986247)
XLA Ops:
  7.2 0.0 reduce-scatter.2.cloned.1.call-start
  7.3 6.2 %convert_element_type.45 = bf16[2048,1024]{1,0:T(8,128)(2,1)} convert(f32[2048,1024]{1,0:T(8,128)} %param.15) | non-fusion elementwise | flops 2097152 | bytes 12582912 | tf_op jit(solution)/shard_map/convert_element_type | solution.py:357
  13.5 0.8 fusion.23
  14.3 1.5 fusion.46
  15.8 1.6 fusion.20
  17.5 0.5 copy-done.17
  18.0 1.2 copy.31.att_ref
  19.1 76.6 %shard_map.170 = (bf16[4,2,384,1024]{3,2,1,0:T(8,128)(2,1)}, bf16[4,384,1024]{2,1,0:T(8,128)(2,1)}) custom-call(bf16[384,1024]{1,0:T(8,128)(2,1)} %grad_ref.1, bf16[384,1024]{1,0:T(8,128)(2,1)} %copy.31.att_ref), custom_call_target="tpu_custom_call" | custom-call | tf_op jit(solution)/shard_map/pallas_call | solution.py:254
  95.8 4.2 %fusion.43 = (bf16[4,1,384,1024]{3,2,1,0:T(8,128)(2,1)S(1)}, bf16[4,1,384,1024]{3,2,1,0:T(8,128)(2,1)S(1)}) fusion(bf16[4,2,384,1024]{3,2,1,0:T(8,128)(2,1)} %get-tuple-element.14), kind=kLoop, calls=%fused_computation.53 | loop fusion | bytes 12582912 | tf_op jit(solution)/shard_map/slice | solution.py:375
  100.0 3.5 %fusion.16 = f32[1536,1024]{1,0:T(8,128)S(1)} fusion(bf16[1536,1024]{1,0:T(8,128)(2,1)S(1)} %bitcast.71, bf16[2048,1024]{1,0:T(8,128)(2,1)S(1)} %copy-done.3), kind=kOutput, calls=%fused_computation.29 | convolution fusion | flops 3221225472 | bytes 11534336 | tf_op jit(solution)/shard_map/dot_general | solution.py:377
  103.5 5.1 %add_convert_fusion = bf16[1536,1024]{1,0:T(8,128)(2,1)} fusion(f32[1536,1024]{1,0:T(8,128)S(1)} %fusion.16, bf16[1536,1024]{1,0:T(8,128)(2,1)S(1)} %bitcast.73, bf16[2048,1024]{1,0:T(8,128)(2,1)S(1)} %copy-done.3), kind=kOutput, calls=%fused_computation.12 | convolution fusion | flops 3224371200 | bytes 14680064 | tf_op jit(solution)/shard_map/dot_general | solution.py:377
  108.6 6.6 %fusion.48 = f32[1024,1024]{1,0:T(8,128)S(1)} fusion(bf16[1536,1024]{1,0:T(8,128)(2,1)} %bitcast.74, bf16[1536,1024]{1,0:T(8,128)(2,1)} %bitcast.89), kind=kOutput, calls=%fused_computation.58 | convolution fusion | flops 3221225472 | bytes 10485760 | tf_op jit(solution)/shard_map/sc,sh->ch/dot_general | solution.py:390
  115.3 3.5 %fusion.47 = f32[1024,1024]{1,0:T(8,128)S(1)} fusion(bf16[1536,1024]{1,0:T(8,128)(2,1)S(1)} %bitcast.72, bf16[1536,1024]{1,0:T(8,128)(2,1)S(1)} %bitcast.90), kind=kOutput, calls=%fused_computation.57 | convolution fusion | flops 3221225472 | bytes 10485760 | tf_op jit(solution)/shard_map/sc,sh->ch/dot_general | solution.py:390
  118.9 10.8 %abs_reduce_fusion.2 = (f32[1024]{0:T(1024)S(1)}, f32[2048]{0:T(1024)S(1)}, f32[2048,1024]{1,0:T(8,128)}, f32[2048]{0:T(1024)S(1)}, f32[1024]{0:T(1024)S(1)}, /*index=5*/f32[2048,1024]{1,0:T(8,128)}) fusion(f32[1024,1024]{1,0:T(8,128)S(1)} %fusion.48, f32[1024,1024]{1,0:T(8,128)S(1)} %fusion.47, f32[1024]{0:T(1024)S(1)} %copy-done.14, ...), kind=kLoop, calls=%fused_computation.10 | loop fusion | flops 41936896 | bytes 33603584 | tf_op jit(solution)/shard_map/reduce_max | solution.py:407
  129.7 0.6 pad_maximum_fusion.2.c_ref
  130.4 0.6 pad_maximum_fusion.1.r_ref
  131.0 17.5 %shard_map.171 = (f32[2,2048]{1,0:T(2,128)}, f32[2,1024]{1,0:T(2,128)}) custom-call(f32[2,2048]{1,0:T(2,128)} %pad_maximum_fusion.1.r_ref, f32[2,1024]{1,0:T(2,128)} %pad_maximum_fusion.2.c_ref), custom_call_target="tpu_custom_call" | custom-call | tf_op jit(solution)/shard_map/pallas_call | solution.py:317
  148.5 0.8 fusion.45
  149.3 0.8 fusion.44
  150.2 20.5 %divide_convert_fusion = (bf16[2048,1024]{1,0:T(8,128)(2,1)}, f32[2048,1024]{1,0:T(8,128)}, bf16[2048,1024]{1,0:T(8,128)(2,1)}) fusion(f32[2048,1024]{1,0:T(8,128)} %get-tuple-element.39, f32[1024]{0:T(1024)S(1)} %bitcast.84, f32[2048]{0:T(1024)S(1)} %bitcast.78, f32[2048,1024]{1,0:T(8,128)} %param.15, f32[2048,1024]{1,0:T(8,128)} %get-tuple-element.32, ...), kind=kLoop, calls=%fused_computation.4 | loop fusion | flops 33554432 | bytes 41967616 | tf_op jit(solution)/shard_map/convert_element_type | solution.py:414
  170.8 1.5 copy.23
  172.3 0.2 multiply_reduce_fusion
  172.5 3.6 %multiply_convert_fusion = bf16[128,8,384]{2,0,1:T(8,128)(2,1)S(1)} fusion(bf16[384,8,128]{0,2,1:T(8,128)(2,1)S(1)} %bitcast.70, f32[8,384]{1,0:T(8,128)S(1)} %bitcast.88, f32[8,384,384]{1,2,0:T(8,128)} %copy-done.17, f32[8,384]{1,0:T(8,128)S(1)} %get-tuple-element.46, bf16[384,1024]{1,0:T(8,128)(2,1)} %param.13, s32[]{:T(128)S(6)} %select_n.14, ...), kind=kOutput, calls=%fused_computation.31 | convolution fusion | flops 609484800 | bytes 6513664 | tf_op jit(solution)/shard_map/hqk,kd->qhd/dot_general | solution.py:57
  176.1 1.2 copy.26
  (38 shorter events, 0.2 us)
Async XLA Ops:
  7.2 6.3 %copy-start = (bf16[384,1024]{1,0:T(8,128)(2,1)S(1)}, bf16[384,1024]{1,0:T(8,128)(2,1)}, u32[]{:S(2)}) copy-start(bf16[384,1024]{1,0:T(8,128)(2,1)} %param.12) | copy-start | bytes 2359300
  7.2 163.6 %reduce-scatter.2.cloned.1.call-start = ((), (), s32[]{:S(2)}) async-start(), calls=%async_computation.1 | async-start | bytes 3932160 | tf_op jit(solution)/shard_map/reduce_scatter | solution.py:385
  7.3 6.2 %copy-start.7 = (bf16[384,1024]{1,0:T(8,128)(2,1)S(1)}, bf16[384,1024]{1,0:T(8,128)(2,1)}, u32[]{:S(2)}) copy-start(bf16[384,1024]{1,0:T(8,128)(2,1)} %param.11) | copy-start | bytes 2359300
  15.8 2.1 %copy-start.17 = (f32[8,384,384]{1,2,0:T(8,128)}, f32[8,384,384]{1,2,0:T(8,128)S(1)}, u32[]{:S(2)}) copy-start(f32[8,384,384]{1,2,0:T(8,128)S(1)} %get-tuple-element.47) | copy-start | bytes 14155780
  95.7 4.3 %copy-start.3 = (bf16[2048,1024]{1,0:T(8,128)(2,1)S(1)}, bf16[2048,1024]{1,0:T(8,128)(2,1)}, u32[]{:S(2)}) copy-start(bf16[2048,1024]{1,0:T(8,128)(2,1)} %convert_element_type.45) | copy-start | bytes 12582916
  100.0 3.5 %copy-start.4 = (bf16[4,1,384,1024]{3,2,1,0:T(8,128)(2,1)}, bf16[4,1,384,1024]{3,2,1,0:T(8,128)(2,1)S(1)}, u32[]{:S(2)}) copy-start(bf16[4,1,384,1024]{3,2,1,0:T(8,128)(2,1)S(1)} %get-tuple-element.41) | copy-start | bytes 9437188
  100.0 3.5 %copy-start.6 = (bf16[4,1,384,1024]{3,2,1,0:T(8,128)(2,1)}, bf16[4,1,384,1024]{3,2,1,0:T(8,128)(2,1)S(1)}, u32[]{:S(2)}) copy-start(bf16[4,1,384,1024]{3,2,1,0:T(8,128)(2,1)S(1)} %get-tuple-element.40) | copy-start | bytes 9437188
  108.6 6.6 %copy-start.5 = (bf16[4,1,384,1024]{3,2,1,0:T(8,128)(2,1)S(1)}, bf16[4,1,384,1024]{3,2,1,0:T(8,128)(2,1)}, u32[]{:S(2)}) copy-start(bf16[4,1,384,1024]{3,2,1,0:T(8,128)(2,1)} %copy-done.4) | copy-start | bytes 9437188
  108.6 6.6 %copy-start.16 = (bf16[4,384,1024]{2,1,0:T(8,128)(2,1)S(1)}, bf16[4,384,1024]{2,1,0:T(8,128)(2,1)}, u32[]{:S(2)}) copy-start(bf16[4,384,1024]{2,1,0:T(8,128)(2,1)} %get-tuple-element.15) | copy-start | bytes 9437188
  115.2 3.6 %copy-start.1 = (bf16[2048,1024]{1,0:T(8,128)(2,1)S(1)}, bf16[2048,1024]{1,0:T(8,128)(2,1)}, u32[]{:S(2)}) copy-start(bf16[2048,1024]{1,0:T(8,128)(2,1)} %param.16) | copy-start | bytes 12582916
  115.3 3.6 %copy-start.2 = (bf16[2048,1024]{1,0:T(8,128)(2,1)S(1)}, bf16[2048,1024]{1,0:T(8,128)(2,1)}, u32[]{:S(2)}) copy-start(bf16[2048,1024]{1,0:T(8,128)(2,1)} %param.19) | copy-start | bytes 12582916
  115.3 3.6 %copy-start.12 = (f32[2048]{0:T(1024)S(1)}, f32[2048]{0:T(1024)}, u32[]{:S(2)}) copy-start(f32[2048]{0:T(1024)} %param.17) | copy-start | bytes 24580
  115.3 3.6 %copy-start.13 = (f32[2048]{0:T(1024)S(1)}, f32[2048]{0:T(1024)}, u32[]{:S(2)}) copy-start(f32[2048]{0:T(1024)} %param.20) | copy-start | bytes 24580
  115.3 3.6 %copy-start.14 = (f32[1024]{0:T(1024)S(1)}, f32[1024]{0:T(1024)}, u32[]{:S(2)}) copy-start(f32[1024]{0:T(1024)} %param.18) | copy-start | bytes 12292
  115.3 3.6 %copy-start.15 = (f32[1024]{0:T(1024)S(1)}, f32[1024]{0:T(1024)}, u32[]{:S(2)}) copy-start(f32[1024]{0:T(1024)} %param.21) | copy-start | bytes 12292
  149.3 21.4 %copy-start.10 = (f32[1,1024]{1,0:T(1,128)}, f32[1,1024]{1,0:T(1,128)S(1)}, u32[]{:S(2)}) copy-start(f32[1,1024]{1,0:T(1,128)S(1)} %get-tuple-element.44) | copy-start | bytes 12292
  149.3 21.4 %copy-start.11 = (f32[1,1024]{1,0:T(1,128)}, f32[1,1024]{1,0:T(1,128)S(1)}, u32[]{:S(2)}) copy-start(f32[1,1024]{1,0:T(1,128)S(1)} %get-tuple-element.45) | copy-start | bytes 12292
  150.2 20.6 %copy-start.8 = (f32[1,2048]{1,0:T(1,128)}, f32[1,2048]{1,0:T(1,128)S(1)}, u32[]{:S(2)}) copy-start(f32[1,2048]{1,0:T(1,128)S(1)} %get-tuple-element.42) | copy-start | bytes 24580
  150.2 20.6 %copy-start.9 = (f32[1,2048]{1,0:T(1,128)}, f32[1,2048]{1,0:T(1,128)S(1)}, u32[]{:S(2)}) copy-start(f32[1,2048]{1,0:T(1,128)S(1)} %get-tuple-element.43) | copy-start | bytes 24580
Sparse Core Ops, SparseCore 0:
  108.7 53.1 reduce-scatter.1
